TPU v7x, 256 devices: a whole 4x4x8 slice. The times are simulated.
256 devices in a mesh: dp: 32 (over z_lo, x, core), feat: 8 (over y, z_hi).
Axes of the slice: x: 4, y: 4, z: 8 (z_hi: 2, z_lo: 4; z = z_hi * 4 + z_lo), core: 2. Of those that a mesh axis runs over, the one named last changes fastest.
Arguments:
- view_a: bfloat16 [4096, 4096], P('dp', 'feat'), may hold values from -24 to 24
- view_b: bfloat16 [4096, 4096], P('dp', 'feat'), may hold values from -24 to 24
Outputs:
- grad_a: bfloat16 [4096, 4096], P('dp', 'feat')
- grad_b: bfloat16 [4096, 4096], P('dp', 'feat')
- loss: float32 [], replicated
All inputs are finite; a program needn't handle non-finite values.
Results may differ from a plain program's by a relative error of at most 0.0068.
Values may be sent and summed in bfloat16 or wider, within the bound.
A program may use at most 64 MiB of HBM per device.

v0:
```python
import jax
import jax.numpy as jnp
from jax import lax
from jax.sharding import Mesh
from jax.sharding import PartitionSpec as P

F = 4096
DP = ("dp_0", "dp_1", "dp_2")
FEAT = ("feat_0", "feat_1")
DP_FEAT = ("dp_0", "dp_1", "dp_2", "feat_0", "feat_1")
EPS = 1e-05
LAMBDA = 0.0051


def from_everyone(x, axis):
    copies = jnp.broadcast_to(x, (lax.axis_size(axis), *x.shape))
    return lax.all_to_all(copies, axis, split_axis=0, concat_axis=0, tiled=True)


def of_everyone(x, axis):
    return from_everyone(x, axis).sum(axis=0)


def in_one(arrays, axis):
    line, at, gathered = (jnp.concatenate([a.reshape(-1) for a in arrays]), 0, [])
    running = of_everyone(line, axis)
    for a in arrays:
        gathered.append(running[at : at + a.size].reshape(a.shape))
        at += a.size
    return tuple(gathered)


def joined_along(parts, dim):
    parts = jnp.moveaxis(parts, 0, dim)
    dims = parts.shape
    return parts.reshape(*dims[:dim], dims[dim] * dims[dim + 1], *dims[dim + 2 :])


def collect(x, axis, dim):
    parts = from_everyone(x, axis)
    return joined_along(parts, dim)


def split_up(x, dim, length):
    before, after = (x.shape[:dim], x.shape[dim + 1 :])
    return jnp.moveaxis(x.reshape(*before, length, -1, *after), dim, 0)


def scatter_pairs(x, chips, core, dim):
    sizes = (lax.axis_size(chips), lax.axis_size(core))
    parts = split_up(x, dim, sizes[0] * sizes[1])
    inside = parts.shape[1:]
    parts = parts.reshape(*sizes, *inside).swapaxes(0, 1).reshape(-1, *inside)
    parts = lax.psum_scatter(parts, core, scatter_dimension=0, tiled=True)
    return lax.psum_scatter(parts, chips, scatter_dimension=0, tiled=True)[0]


def over_axes(x, axes):
    for axis in axes:
        x = lax.psum(x, axis)
    return x


def shards(view_a, view_b):
    rows, local = view_a.shape
    groups = lax.axis_size(DP)
    count = rows * groups
    vals_a = view_a.astype(jnp.float32)
    vals_b = view_b.astype(jnp.float32)
    sums = in_one(
        (
            jnp.sum(vals_a, axis=0),
            jnp.sum(vals_a * vals_a, axis=0),
            jnp.sum(vals_b, axis=0),
            jnp.sum(vals_b * vals_b, axis=0),
        ),
        DP,
    )
    center_a = sums[0] / count
    center_b = sums[2] / count
    inverse_a = lax.rsqrt(sums[1] / count - center_a * center_a + EPS)
    inverse_b = lax.rsqrt(sums[3] / count - center_b * center_b + EPS)
    normed_a = (vals_a - center_a) * inverse_a
    normed_b = (vals_b - center_b) * inverse_b
    a_half = normed_a.astype(jnp.bfloat16)
    b_half = normed_b.astype(jnp.bfloat16)
    b_every = collect(b_half, FEAT, 1)
    block_rows = F // groups
    corr_t = (
        scatter_pairs(
            lax.dot_general(
                b_every, a_half, (((0,), (0,)), ((), ())), preferred_element_type=jnp.float32
            ),
            ("dp_0", "dp_1"),
            "dp_2",
            0,
        )
        / count
    )
    row_ids = lax.axis_index(DP) * block_rows + lax.broadcasted_iota(
        jnp.int32, (block_rows, local), 0
    )
    col_ids = lax.axis_index(FEAT) * local + lax.broadcasted_iota(jnp.int32, (block_rows, local), 1)
    unit = (row_ids == col_ids).astype(jnp.float32)
    partial_loss = jnp.sum(unit * (1.0 - corr_t) ** 2) + LAMBDA * jnp.sum(
        (1.0 - unit) * corr_t * corr_t
    )
    loss = over_axes(partial_loss, DP_FEAT) / F
    grad_t = (unit * (-2.0 * (1.0 - corr_t)) + (1.0 - unit) * (2.0 * LAMBDA) * corr_t).astype(
        jnp.bfloat16
    )
    grad_full = lax.all_gather(grad_t, DP, axis=0, tiled=True)
    grad_na = jnp.dot(b_every, grad_full, preferred_element_type=jnp.float32)
    partial_b = lax.dot_general(
        a_half, grad_full, (((1,), (1,)), ((), ())), preferred_element_type=jnp.float32
    )
    grad_nb = lax.psum_scatter(partial_b, FEAT, scatter_dimension=1, tiled=True)
    stats = in_one(
        (
            jnp.sum(grad_na, axis=0),
            jnp.sum(grad_na * normed_a, axis=0),
            jnp.sum(grad_nb, axis=0),
            jnp.sum(grad_nb * normed_b, axis=0),
        ),
        DP,
    )
    grad_a = (inverse_a * (grad_na - stats[0] / count - normed_a * (stats[1] / count))).astype(
        jnp.bfloat16
    )
    grad_b = (inverse_b * (grad_nb - stats[2] / count - normed_b * (stats[3] / count))).astype(
        jnp.bfloat16
    )
    return (grad_a, grad_b, loss)


def solution(mesh):
    torus = Mesh(mesh.devices.reshape(4, 4, 2, 4, 2), ("dp_0", "dp_1", "dp_2", "feat_0", "feat_1"))
    in_specs = (P(DP, FEAT), P(DP, FEAT))
    out_specs = (P(DP, FEAT), P(DP, FEAT), P())
    return jax.shard_map(
        shards, mesh=torus, in_specs=in_specs, out_specs=out_specs, check_vma=False
    )
```

profile of v0, /device:TPU:0, one launch (start us, length us, event | category | flops | bytes accessed | tf_op | source)
XLA Modules:
  0.0 412.7 jit_solution(12478503057353456559)
XLA Ops:
  7.2 0.0 reduce-scatter.4.cloned.1.call-start
  7.2 1.1 convert_reduce_fusion
  8.3 0.1 broadcast_in_dim.6
  8.5 17.9 %all_to_all.17 = f32[32,1,2048]{2,1,0:T(1,128)S(1)} all-to-all(f32[32,1,2048]{2,1,0:T(1,128)S(1)} %broadcast_in_dim.6), channel_id=1, replica_groups=mesh['dp_0'=4,'dp_1'=4,'dp_2'=2,'feat_0'=4,'feat_1'=2] {'dp_0','dp_1','d..., dimensions={0} | all-to-all | bytes 524288 | tf_op jit(solution)/shard_map/all_to_all | solution.py:17
  26.4 0.2 reduce_sum.112
  26.6 0.9 fusion.13
  27.5 0.1 copy.11
  27.6 0.1 broadcast_in_dim.7
  27.8 34.1 %all_to_all.18 = bf16[8,128,512]{1,2,0:T(8,128)(2,1)S(1)} all-to-all(bf16[8,128,512]{1,2,0:T(8,128)(2,1)S(1)} %broadcast_in_dim.7), channel_id=1, replica_groups=mesh['dp_0'=4,'dp_1'=4,'dp_2'=2,'feat_0'=4,'feat_1'=2] {'feat_0','feat_1'}, dimensions={0} | all-to-all | bytes 2097152 | tf_op jit(solution)/shard_map/all_to_all | solution.py:17
  61.9 1.3 convolution_bitcast_fusion
  63.1 4.2 %copy.12 = f32[2,16,128,512]{3,2,1,0:T(8,128)} copy(f32[2,16,128,512]{3,2,0,1:T(8,128)S(1)} %convolution_bitcast_fusion) | data formatting | bytes 16777216 | tf_op jit(solution)/shard_map/transpose | solution.py:53
  67.4 0.0 reduce-scatter.6.cloned.1.call-start
  67.5 19.9 %reduce-scatter.4.cloned.1.call-done = f32[16,128,512]{2,1,0:T(8,128)} async-done(((f32[32,128,512]{2,1,0:T(8,128)}), f32[16,128,512]{2,1,0:T(8,128)}) %reduce-scatter.4.cloned.1.call-update) | async-done | bytes 4194320 | tf_op jit(solution)/shard_map/reduce_scatter | solution.py:54
  87.4 0.0 all-gather.2.cloned.1.call-start
  87.5 98.5 %reduce-scatter.6.cloned.1.call-done = f32[1,128,512]{2,1,0:T(8,128)} async-done(((f32[16,128,512]{2,1,0:T(8,128)}), f32[1,128,512]{2,1,0:T(8,128)}) %reduce-scatter.6.cloned.1.call-update) | async-done | bytes 262160 | tf_op jit(solution)/shard_map/reduce_scatter | solution.py:55
  186.0 2.4 fusion.18
  188.4 0.0 reduce-scatter.8.cloned.1.call-start
  188.5 58.6 %all-gather.2.cloned.1.call-done = bf16[4096,512]{1,0:T(8,128)(2,1)} async-done(((bf16[128,512]{1,0:T(8,128)(2,1)}), bf16[4096,512]{1,0:T(8,128)(2,1)}) %all-gather.2.cloned.1.call-update) | async-done | bytes 4194320 | tf_op jit(solution)/shard_map/all_gather | solution.py:112
  247.1 5.0 %fusion.26 = f32[128,4096]{1,0:T(8,128)} fusion(bf16[4096,512]{1,0:T(8,128)(2,1)} %all-gather.2.cloned.1.call-done, bf16[128,512]{1,0:T(8,128)(2,1)S(1)} %copy-done, f32[512]{0:T(512)S(1)} %get-tuple-element.20, f32[512]{0:T(512)S(1)} %get-tuple-element.18), kind=kOutput, calls=%fused_computation.38 | convolution fusion | flops 537133056 | bytes 6426624 | tf_op jit(solution)/shard_map/dot_general | solution.py:114
  252.1 3.0 fusion.35
  255.1 91.8 %reduce-scatter.8.cloned.1.call-done = f32[128,512]{1,0:T(8,128)} async-done(((f32[128,4096]{1,0:T(8,128)}), f32[128,512]{1,0:T(8,128)}) %reduce-scatter.8.cloned.1.call-update) | async-done | bytes 262160 | tf_op jit(solution)/shard_map/reduce_scatter | solution.py:117
  346.9 1.0 fusion.36
  347.9 0.8 broadcast_in_dim.8
  348.8 4.9 %all-to-all-start.2 = ((f32[32,1,2048]{2,1,0:T(1,128)}), f32[32,1,2048]{2,1,0:T(1,128)S(1)}, u32[]{:S(2)}, u32[]{:S(2)}) async-start(f32[32,1,2048]{2,1,0:T(1,128)} %broadcast_in_dim.8), calls=%async_computation.5 | async-start | bytes 524288 | tf_op jit(solution)/shard_map/all_to_all | solution.py:17
  355.0 12.5 %psum.35 = f32[]{:T(128)} all-reduce(f32[]{:T(128)S(6)} %add.61), channel_id=1, replica_groups=mesh['dp_0'=4,'dp_1'=4,'dp_2'=2,'feat_0'=4,'feat_1'=2] {'dp_0'}, use_global_device_ids=true, to_apply=%region_15.0 | all-reduce | flops 1 | bytes 8 | tf_op jit(solution)/shard_map/psum | solution.py:60
  367.5 11.0 %psum.36 = f32[]{:T(128)} all-reduce(f32[]{:T(128)} %psum.35), channel_id=1, replica_groups=mesh['dp_0'=4,'dp_1'=4,'dp_2'=2,'feat_0'=4,'feat_1'=2] {'dp_1'}, use_global_device_ids=true, to_apply=%region_16.0 | all-reduce | flops 1 | bytes 8 | tf_op jit(solution)/shard_map/psum | solution.py:60
  378.5 3.1 psum.37
  381.6 10.7 %psum.38 = f32[]{:T(128)} all-reduce(f32[]{:T(128)} %psum.37), channel_id=1, replica_groups=mesh['dp_0'=4,'dp_1'=4,'dp_2'=2,'feat_0'=4,'feat_1'=2] {'feat_0'}, use_global_device_ids=true, to_apply=%region_18.0 | all-reduce | flops 1 | bytes 8 | tf_op jit(solution)/shard_map/psum | solution.py:60
  392.4 9.4 %psum.39 = f32[]{:T(128)} all-reduce(f32[]{:T(128)} %psum.38), channel_id=1, replica_groups=mesh['dp_0'=4,'dp_1'=4,'dp_2'=2,'feat_0'=4,'feat_1'=2] {'feat_1'}, use_global_device_ids=true, to_apply=%region_19.0 | all-reduce | flops 1 | bytes 8 | tf_op jit(solution)/shard_map/psum | solution.py:60
  402.5 0.2 reduce_sum.117
  402.7 0.7 fusion.8
  403.4 1.7 fusion.17
  (15 shorter events, 0.1 us)
Async XLA Ops:
  7.2 54.7 %copy-start = (bf16[128,512]{1,0:T(8,128)(2,1)S(1)}, bf16[128,512]{1,0:T(8,128)(2,1)}, u32[]{:S(2)}) copy-start(bf16[128,512]{1,0:T(8,128)(2,1)} %param.2) | copy-start | bytes 393220
  7.2 80.2 %reduce-scatter.4.cloned.1.call-start = ((), (), s32[]{:S(2)}) async-start(), calls=%async_computation.6 | async-start | bytes 12582912 | tf_op jit(solution)/shard_map/reduce_scatter | solution.py:54
  67.4 118.6 %reduce-scatter.6.cloned.1.call-start = ((), (), s32[]{:S(2)}) async-start(), calls=%async_computation.7 | async-start | bytes 4456448 | tf_op jit(solution)/shard_map/reduce_scatter | solution.py:55
  87.4 159.7 %all-gather.2.cloned.1.call-start = ((), (), s32[]{:S(2)}) async-start(), calls=%async_computation.8 | async-start | bytes 4325376 | tf_op jit(solution)/shard_map/all_gather | solution.py:112
  188.4 158.5 %reduce-scatter.8.cloned.1.call-start = ((), (), s32[]{:S(2)}) async-start(), calls=%async_computation.9 | async-start | bytes 2359296 | tf_op jit(solution)/shard_map/reduce_scatter | solution.py:117
  252.1 94.8 %copy-start.1 = (bf16[128,512]{1,0:T(8,128)(2,1)S(1)}, bf16[128,512]{1,0:T(8,128)(2,1)}, u32[]{:S(2)}) copy-start(bf16[128,512]{1,0:T(8,128)(2,1)} %param.3) | copy-start | bytes 393220
  348.8 53.7 %all-to-all-start.2 = ((f32[32,1,2048]{2,1,0:T(1,128)}), f32[32,1,2048]{2,1,0:T(1,128)S(1)}, u32[]{:S(2)}, u32[]{:S(2)}) async-start(f32[32,1,2048]{2,1,0:T(1,128)} %broadcast_in_dim.8), calls=%async_computation.5 | async-start | bytes 524288 | tf_op jit(solution)/shard_map/all_to_all | solution.py:17
Sparse Core Ops, SparseCore 0:
  67.5 19.8 reduce-scatter.3
  89.9 96.0 reduce-scatter.5
  188.6 58.5 all-gather.1
  252.3 94.5 reduce-scatter.7
where the time goes:
time: 413 us
  waiting for transfers between devices  269 us (65%)
  blocking collectives  98.9 us (24%)
  between operations  17 us (4%)
  matrix products  9.23 us (2%)
  other arithmetic  8.25 us (2%)
  local copies, waits for them, and re-layouts  5.46 us (1%)
  starting transfers between devices  5.08 us (1%)
    reduce_scatter x1, waiting for transfers between devices, scatter_pairs(): return lax.psum_scatter(parts, chips, scatter_dimension=0, tiled=True)[0]  98.5 us
    reduce_scatter x1, waiting for transfers between devices, shards(): grad_nb = lax.psum_scatter(partial_b, FEAT, scatter_dimension=1, tiled=True)  91.8 us
    all_gather x1, waiting for transfers between devices, shards(): grad_full = lax.all_gather(grad_t, DP, axis=0, tiled=True)  58.6 us
    all_to_all x2, blocking collectives, from_everyone(): return lax.all_to_all(copies, axis, split_axis=0, concat_axis=0, tiled=True)  52 us
    psum x5, blocking collectives, over_axes(): x = lax.psum(x, axis)  46.8 us
    reduce_scatter x1, waiting for transfers between devices, scatter_pairs(): parts = lax.psum_scatter(parts, core, scatter_dimension=0, tiled=True)  19.9 us
  transfers between devices with their start and end apart: 5, of which 4 were waited for; matrix products, arithmetic and copies ran while one was open for 1% of the time, Pallas kernels for 0%

commit v1 on v0

--- a/solution.py
+++ b/solution.py
@@ -109,7 +109,9 @@
     grad_t = (unit * (-2.0 * (1.0 - corr_t)) + (1.0 - unit) * (2.0 * LAMBDA) * corr_t).astype(
         jnp.bfloat16
     )
-    grad_full = lax.all_gather(grad_t, DP, axis=0, tiled=True)
+    grad_full = jnp.concatenate(
+        lax.all_to_all(jnp.stack([grad_t] * lax.axis_size(DP)), DP, 0, 0), axis=0
+    )
     grad_na = jnp.dot(b_every, grad_full, preferred_element_type=jnp.float32)
     partial_b = lax.dot_general(
         a_half, grad_full, (((1,), (1,)), ((), ())), preferred_element_type=jnp.float32

time: 413 us -> 452 us (1.094)
  blocking collectives: 98.9 us -> 196 us
  waiting for transfers between devices: 269 us -> 211 us
    all_to_all x0 -> x1, blocking collectives: none -> 96.7 us  [shards(): lax.all_to_all(jnp.stack([grad_t] * lax.axis_size(DP)), DP, 0, 0)]
    all_gather x1 -> x0, waiting for transfers between devices: 58.6 us -> none  [shards(): grad_full = lax.all_gather(grad_t, DP, axis=0, tiled=True)]
  transfers between devices with their start and end apart: 5 -> 4, of which waited for: 4 -> 3; matrix products, arithmetic and copies ran while one was open for 1% -> 1% of each run, Pallas kernels for 0% -> 0%
where the time goes in v1:
time: 452 us
  waiting for transfers between devices  211 us (47%)
  blocking collectives  196 us (43%)
  between operations  17 us (4%)
  local copies, waits for them, and re-layouts  7.85 us (2%)
  other arithmetic  7.73 us (2%)
  matrix products  7.07 us (2%)
  starting transfers between devices  5.01 us (1%)
    reduce_scatter x1, waiting for transfers between devices, scatter_pairs(): return lax.psum_scatter(parts, chips, scatter_dimension=0, tiled=True)[0]  98.5 us
    all_to_all x1, blocking collectives, shards(): lax.all_to_all(jnp.stack([grad_t] * lax.axis_size(DP)), DP, 0, 0)  96.7 us
    reduce_scatter x1, waiting for transfers between devices, shards(): grad_nb = lax.psum_scatter(partial_b, FEAT, scatter_dimension=1, tiled=True)  92.9 us
    all_to_all x2, blocking collectives, from_everyone(): return lax.all_to_all(copies, axis, split_axis=0, concat_axis=0, tiled=True)  52 us
    psum x5, blocking collectives, over_axes(): x = lax.psum(x, axis)  46.8 us
    reduce_scatter x1, waiting for transfers between devices, scatter_pairs(): parts = lax.psum_scatter(parts, core, scatter_dimension=0, tiled=True)  19.9 us
  transfers between devices with their start and end apart: 4, of which 3 were waited for; matrix products, arithmetic and copies ran while one was open for 1% of the time, Pallas kernels for 0%

profile of v1, /device:TPU:0, one launch (start us, length us, event | category | flops | bytes accessed | tf_op | source)
XLA Modules:
  0.0 451.6 jit_solution(17510807596026867051)
XLA Ops:
  7.2 1.1 convert_reduce_fusion
  8.3 0.1 broadcast_in_dim.6
  8.5 17.9 %all_to_all.22 = f32[32,1,2048]{2,1,0:T(1,128)S(1)} all-to-all(f32[32,1,2048]{2,1,0:T(1,128)S(1)} %broadcast_in_dim.6), channel_id=1, replica_groups=mesh['dp_0'=4,'dp_1'=4,'dp_2'=2,'feat_0'=4,'feat_1'=2] {'dp_0','dp_1','d..., dimensions={0} | all-to-all | bytes 524288 | tf_op jit(solution)/shard_map/all_to_all | solution.py:17
  26.4 0.2 reduce_sum.112
  26.6 0.9 fusion.20
  27.5 0.1 copy.11
  27.6 0.1 broadcast_in_dim.7
  27.8 34.1 %all_to_all.23 = bf16[8,128,512]{1,2,0:T(8,128)(2,1)S(1)} all-to-all(bf16[8,128,512]{1,2,0:T(8,128)(2,1)S(1)} %broadcast_in_dim.7), channel_id=1, replica_groups=mesh['dp_0'=4,'dp_1'=4,'dp_2'=2,'feat_0'=4,'feat_1'=2] {'feat_0','feat_1'}, dimensions={0} | all-to-all | bytes 2097152 | tf_op jit(solution)/shard_map/all_to_all | solution.py:17
  61.9 1.3 convolution_bitcast_fusion
  63.1 4.2 copy.12
  67.4 0.0 reduce-scatter.6.cloned.1.call-start
  67.5 19.9 %reduce-scatter.4.cloned.1.call-done = f32[16,128,512]{2,1,0:T(8,128)} async-done(((f32[32,128,512]{2,1,0:T(8,128)}), f32[16,128,512]{2,1,0:T(8,128)}) %reduce-scatter.4.cloned.1.call-update) | async-done | bytes 4194320 | tf_op jit(solution)/shard_map/reduce_scatter | solution.py:54
  87.5 98.5 %reduce-scatter.6.cloned.1.call-done = f32[1,128,512]{2,1,0:T(8,128)} async-done(((f32[16,128,512]{2,1,0:T(8,128)}), f32[1,128,512]{2,1,0:T(8,128)}) %reduce-scatter.6.cloned.1.call-update) | async-done | bytes 262160 | tf_op jit(solution)/shard_map/reduce_scatter | solution.py:55
  186.0 1.1 fusion.28
  187.1 0.5 stack.5
  187.6 96.7 %all_to_all.24 = bf16[32,128,512]{2,1,0:T(8,128)(2,1)S(1)} all-to-all(bf16[32,128,512]{2,1,0:T(8,128)(2,1)S(1)} %stack.5), channel_id=1, replica_groups=mesh['dp_0'=4,'dp_1'=4,'dp_2'=2,'feat_0'=4,'feat_1'=2] {'dp_0','dp_1','d..., dimensions={0} | all-to-all | bytes 8388608 | tf_op jit(solution)/shard_map/all_to_all | solution.py:113
  284.2 1.9 copy-done
  286.2 2.8 fusion.29
  289.0 3.0 fusion.38
  292.0 92.9 %reduce-scatter.8.cloned.1.call-done = f32[128,512]{1,0:T(8,128)} async-done(((f32[128,4096]{1,0:T(8,128)}), f32[128,512]{1,0:T(8,128)}) %reduce-scatter.8.cloned.1.call-update) | async-done | bytes 262160 | tf_op jit(solution)/shard_map/reduce_scatter | solution.py:119
  384.9 1.0 fusion.39
  386.0 0.8 broadcast_in_dim.8
  386.8 4.9 %all-to-all-start.3 = ((f32[32,1,2048]{2,1,0:T(1,128)}), f32[32,1,2048]{2,1,0:T(1,128)S(1)}, u32[]{:S(2)}, u32[]{:S(2)}) async-start(f32[32,1,2048]{2,1,0:T(1,128)} %broadcast_in_dim.8), calls=%async_computation.6 | async-start | bytes 524288 | tf_op jit(solution)/shard_map/all_to_all | solution.py:17
  391.7 0.8 fusion.25
  393.8 12.5 %psum.35 = f32[]{:T(128)} all-reduce(f32[]{:T(128)S(6)} %add.62), channel_id=1, replica_groups=mesh['dp_0'=4,'dp_1'=4,'dp_2'=2,'feat_0'=4,'feat_1'=2] {'dp_0'}, use_global_device_ids=true, to_apply=%region_15.0 | all-reduce | flops 1 | bytes 8 | tf_op jit(solution)/shard_map/psum | solution.py:60
  406.3 11.0 %psum.36 = f32[]{:T(128)} all-reduce(f32[]{:T(128)} %psum.35), channel_id=1, replica_groups=mesh['dp_0'=4,'dp_1'=4,'dp_2'=2,'feat_0'=4,'feat_1'=2] {'dp_1'}, use_global_device_ids=true, to_apply=%region_16.0 | all-reduce | flops 1 | bytes 8 | tf_op jit(solution)/shard_map/psum | solution.py:60
  417.4 3.1 psum.37
  420.5 10.7 %psum.38 = f32[]{:T(128)} all-reduce(f32[]{:T(128)} %psum.37), channel_id=1, replica_groups=mesh['dp_0'=4,'dp_1'=4,'dp_2'=2,'feat_0'=4,'feat_1'=2] {'feat_0'}, use_global_device_ids=true, to_apply=%region_18.0 | all-reduce | flops 1 | bytes 8 | tf_op jit(solution)/shard_map/psum | solution.py:60
  431.2 9.4 %psum.39 = f32[]{:T(128)} all-reduce(f32[]{:T(128)} %psum.38), channel_id=1, replica_groups=mesh['dp_0'=4,'dp_1'=4,'dp_2'=2,'feat_0'=4,'feat_1'=2] {'feat_1'}, use_global_device_ids=true, to_apply=%region_19.0 | all-reduce | flops 1 | bytes 8 | tf_op jit(solution)/shard_map/psum | solution.py:60
  441.3 0.2 reduce_sum.117
  441.5 0.7 fusion.15
  442.2 1.7 fusion.24
  (19 shorter events, 0.2 us)
Async XLA Ops:
  7.2 54.7 %copy-start.1 = (bf16[128,512]{1,0:T(8,128)(2,1)S(1)}, bf16[128,512]{1,0:T(8,128)(2,1)}, u32[]{:S(2)}) copy-start(bf16[128,512]{1,0:T(8,128)(2,1)} %param.2) | copy-start | bytes 393220
  7.2 80.2 %reduce-scatter.4.cloned.1.call-start = ((), (), s32[]{:S(2)}) async-start(), calls=%async_computation.7 | async-start | bytes 12582912 | tf_op jit(solution)/shard_map/reduce_scatter | solution.py:54
  67.4 118.6 %reduce-scatter.6.cloned.1.call-start = ((), (), s32[]{:S(2)}) async-start(), calls=%async_computation.8 | async-start | bytes 4456448 | tf_op jit(solution)/shard_map/reduce_scatter | solution.py:55
  87.4 297.5 %reduce-scatter.8.cloned.1.call-start = ((), (), s32[]{:S(2)}) async-start(), calls=%async_computation.9 | async-start | bytes 2359296 | tf_op jit(solution)/shard_map/reduce_scatter | solution.py:119
  284.2 1.9 copy-start
  289.0 96.0 %copy-start.2 = (bf16[128,512]{1,0:T(8,128)(2,1)S(1)}, bf16[128,512]{1,0:T(8,128)(2,1)}, u32[]{:S(2)}) copy-start(bf16[128,512]{1,0:T(8,128)(2,1)} %param.3) | copy-start | bytes 393220
  289.0 102.7 %copy-start.3 = (f32[1,128,512]{2,1,0:T(8,128)S(1)}, f32[1,128,512]{2,1,0:T(8,128)}, u32[]{:S(2)}) copy-start(f32[1,128,512]{2,1,0:T(8,128)} %reduce-scatter.6.cloned.1.call-done) | copy-start | bytes 786436
  386.8 54.5 %all-to-all-start.3 = ((f32[32,1,2048]{2,1,0:T(1,128)}), f32[32,1,2048]{2,1,0:T(1,128)S(1)}, u32[]{:S(2)}, u32[]{:S(2)}) async-start(f32[32,1,2048]{2,1,0:T(1,128)} %broadcast_in_dim.8), calls=%async_computation.6 | async-start | bytes 524288 | tf_op jit(solution)/shard_map/all_to_all | solution.py:17
Sparse Core Ops, SparseCore 0:
  67.5 19.8 reduce-scatter.3
  89.9 96.0 reduce-scatter.5
  289.1 95.7 reduce-scatter.7
